TPU v7x, 32 devices: a whole 2x2x4 slice. The times are simulated.
32 devices in a mesh: dp: 8 (over y, x, core), tp: 4 (over z).
Axes of the slice: x: 2, y: 2, z: 4, core: 2. Of those that a mesh axis runs over, the one named last changes fastest.
Arguments:
- inputs: bfloat16 [8, 768, 1280], P('dp', 'tp'), may hold values from -6 to 6
- saved_hidden: bfloat16 [8, 768, 5120], P('dp', None, 'tp'), may hold values from -8 to 8
- upstream: bfloat16 [8, 768, 1280], P('dp', 'tp'), may hold values from -6 to 6
- w_in: bfloat16 [1280, 5120], P(None, 'tp'), may hold values from -0.15625 to 0.15625
- w_out: bfloat16 [5120, 1280], P('tp'), may hold values from -0.078125 to 0.078125
- kernel: float32 [7, 1280], replicated, may hold values from -2 to 2
Outputs:
- grad_inputs: bfloat16 [8, 768, 1280], P('dp', 'tp')
- grad_w_in: float32 [1280, 5120], P(None, 'tp')
- grad_w_out: float32 [5120, 1280], P('tp')
- grad_bias: float32 [5120], P('tp')
- grad_kernel: float32 [7, 1280], replicated
All inputs are finite; a program needn't handle non-finite values.
Results may differ from a plain program's by a relative error of at most 0.02.
Values may be sent and summed in bfloat16 or wider, within the bound.
No kernel may reach another device: no remote copies, remote signals or barrier semaphores. Data moves between devices by JAX's collectives and lax.ppermute only.
A program may use at most 128 MiB of HBM per device.

v0:
```python
import jax
import jax.numpy as jnp
from jax import lax
from jax.sharding import PartitionSpec as P

KW = 7


def with_halo(cells, sides, width):
    for axis, dim in sides:
        count = lax.axis_size(axis)
        ends = count - 1
        head = lax.slice_in_dim(cells, 0, width, axis=dim)
        tail = lax.slice_in_dim(cells, cells.shape[dim] - width, cells.shape[dim], axis=dim)
        cells = jnp.concatenate(
            [
                lax.ppermute(tail, axis, [(i, (i + 1) % count) for i in range(ends)]),
                cells,
                lax.ppermute(head, axis, [((i + 1) % count, i) for i in range(ends)]),
            ],
            axis=dim,
        )
    return cells


def gelu_exact(value):
    return jax.nn.gelu(value, approximate=False)


def convolve(padded, kernel, length):
    mixed = padded[3 : 3 + length].astype(jnp.float32)
    for tap in range(KW):
        mixed = mixed + kernel[tap] * padded[tap : tap + length].astype(jnp.float32)
    return mixed.astype(jnp.bfloat16)


def shards(inputs, saved_hidden, upstream, w_in, w_out, kernel):
    tokens = inputs[0]
    hidden = saved_hidden[0]
    grad_out = upstream[0]
    length = tokens.shape[0]
    piece = lax.all_gather(grad_out, "tp", axis=0, tiled=True)
    hidden_rows = hidden.astype(jnp.float32)
    back_rows = lax.dot_general(
        piece, w_out, (((1,), (1,)), ((), ())), preferred_element_type=jnp.float32
    )
    grad_rows = jax.vjp(gelu_exact, hidden_rows)[1](back_rows)[0].astype(jnp.bfloat16)
    buffer = grad_rows
    activated = gelu_exact(hidden_rows).astype(jnp.bfloat16)
    total = lax.dot_general(
        activated, piece, (((0,), (0,)), ((), ())), preferred_element_type=jnp.float32
    )
    grad_w_out = total
    grad_bias = jnp.sum(buffer.astype(jnp.float32), axis=0)
    summed = lax.psum_scatter(
        lax.dot_general(
            buffer, w_in, (((1,), (1,)), ((), ())), preferred_element_type=jnp.float32
        ).astype(jnp.bfloat16),
        "tp",
        scatter_dimension=0,
        tiled=True,
    ).astype(jnp.float32)
    grad_mixed = (grad_out.astype(jnp.float32) + summed).astype(jnp.bfloat16)
    padded = with_halo(tokens, (("tp", 0),), 3)
    mixed = convolve(padded, kernel, length)
    grad_rows = buffer
    grad_w_in = lax.dot_general(
        lax.all_gather(mixed, "tp", axis=0, tiled=True),
        grad_rows,
        (((0,), (0,)), ((), ())),
        preferred_element_type=jnp.float32,
    )
    grad_pad = with_halo(grad_mixed, (("tp", 0),), 3)
    grad_f = grad_mixed.astype(jnp.float32)
    grad_inputs = grad_f
    taps = []
    for tap in range(KW):
        grad_inputs = grad_inputs + kernel[tap] * grad_pad[6 - tap : 6 - tap + length].astype(
            jnp.float32
        )
        taps.append(jnp.sum(grad_f * padded[tap : tap + length].astype(jnp.float32), axis=0))
    grad_kernel = jnp.stack(taps)
    grad_kernel = lax.psum(grad_kernel, ("dp", "tp"))
    grad_w_in, grad_w_out, grad_bias = (
        lax.psum(grad_w_in.astype(jnp.bfloat16), "dp").astype(jnp.float32),
        lax.psum(grad_w_out.astype(jnp.bfloat16), "dp").astype(jnp.float32),
        lax.psum(grad_bias.astype(jnp.bfloat16), "dp").astype(jnp.float32),
    )
    return (grad_inputs.astype(jnp.bfloat16)[None], grad_w_in, grad_w_out, grad_bias, grad_kernel)


def solution(mesh):
    in_specs = (
        P("dp", "tp", None),
        P("dp", None, "tp"),
        P("dp", "tp", None),
        P(None, "tp"),
        P("tp", None),
        P(),
    )
    out_specs = (P("dp", "tp", None), P(None, "tp"), P("tp", None), P("tp"), P())
    return jax.shard_map(shards, mesh=mesh, in_specs=in_specs, out_specs=out_specs, check_vma=False)
```

profile of v0, /device:TPU:0, one launch (start us, length us, event | category | flops | bytes accessed | tf_op | source)
XLA Modules:
  0.0 318.5 jit_solution(17866380397956469389)
XLA Ops:
  7.2 0.0 copy-start
  7.2 0.0 all-gather.6.cloned.1.call-start
  7.2 0.7 all-gather.6.cloned.1.call-update
  7.9 0.0 all-gather.4.cloned.1.call-start
  8.0 1.0 slice_bitcast_fusion.1
  8.9 5.0 %collective-permute-start.2 = (bf16[3,1280]{1,0:T(4,128)(2,1)S(1)}, bf16[3,1280]{1,0:T(4,128)(2,1)S(1)}, u32[]{:S(2)}, u32[]{:S(2)}) collective-permute-start(bf16[3,1280]{1,0:T(4,128)(2,1)S(1)} %get-tuple-element.27), channel_id=1, source_target_pairs={{0,1},{1,2},{2,3},{4,5},{5,6},{6,7},{8,9},{9,10},{10,11},{12,13},{... | collective-permute-start | bytes 23048 | tf_op jit(solution)/shard_map/ppermute | solution.py:17
  13.9 1.3 collective-permute-start.3
  15.2 1.3 slice_reduce_fusion.6
  16.4 0.0 collective-permute-done.2
  16.5 3.0 collective-permute-done.3
  19.4 4.4 %fusion.52 = bf16[192,1280]{1,0:T(8,128)(2,1)} fusion(bf16[192,1280]{1,0:T(8,128)(2,1)} %bitcast.131, bf16[3,1280]{1,0:T(4,128)(2,1)S(1)} %collective-permute-done.3, bf16[3,1280]{1,0:T(4,128)(2,1)S(1)} %collective-permute-done.2, f32[1280]{0:T(1024)S(1)} %get-tuple-element.20, f32[1280]{0:T(1024)S(1)} %get-tuple-element.21, f32[1280]{0:T(1024)S(1)} %get-tuple-element.16, ...), kind=kLoop, calls=%fused_computation.72 | loop fusion | flops 9830400 | bytes 1034240 | tf_op jit(solution)/shard_map/convert_element_type | solution.py:34
  23.8 0.0 all-gather.4.cloned.1.call-update
  23.9 0.0 all-reduce.3.cloned.1.call-start
  23.9 10.1 %fusion.38 = f32[768,1280]{1,0:T(8,128)} fusion(bf16[1,768,1280]{2,1,0:T(8,128)(2,1)} %param.7), kind=kLoop, calls=%fused_computation.43 | loop fusion | flops 61931520 | bytes 5898240 | tf_op jit(solution)/shard_map/jvp()/erfc | solution.py:27
  34.0 21.8 %all-gather.6.cloned.1.call-done = bf16[1,768,1280]{2,1,0:T(8,128)(2,1)} async-done(((bf16[1,192,1280]{2,1,0:T(8,128)(2,1)}), bf16[1,768,1280]{2,1,0:T(8,128)(2,1)}) %all-gather.6.cloned.1.call-update) | async-done | bytes 1966096 | tf_op jit(solution)/shard_map/all_gather | solution.py:42
  55.8 0.0 copy-start.1
  55.8 0.0 copy-start.4
  55.8 0.0 copy-start.5
  55.8 7.9 %convolution_convert_fusion = bf16[1280,1280]{1,0:T(8,128)(2,1)} fusion(f32[768,1280]{1,0:T(8,128)} %fusion.38, bf16[1,768,1280]{2,1,0:T(8,128)(2,1)} %param.7, bf16[1,768,1280]{2,1,0:T(8,128)(2,1)} %all-gather.6.cloned.1.call-done), kind=kOutput, calls=%fused_computation | convolution fusion | flops 2522152960 | bytes 11141120 | tf_op jit(solution)/shard_map/dot_general | solution.py:50
  63.7 0.0 copy-done
  63.7 0.0 copy-done.1
  63.7 0.0 copy-done.4
  63.7 0.0 copy-done.5
  63.8 4.7 %fusion.80 = (bf16[1280]{0:T(1024)(128)(2,1)S(1)}, bf16[768,1280]{1,0:T(8,128)(2,1)}) fusion(f32[768,1280]{1,0:T(8,128)S(1)} %copy-done.1, bf16[1280,1280]{1,0:T(8,128)(2,1)S(1)} %copy-done, bf16[1,768,1280]{2,1,0:T(8,128)(2,1)S(1)} %copy-done.5, bf16[1,768,1280]{2,1,0:T(8,128)(2,1)S(1)} %copy-done.4), kind=kOutput, calls=%fused_computation.121 | convolution fusion | flops 2532309760 | bytes 13109760 | tf_op jit(solution)/shard_map/dot_general | solution.py:44
  68.5 31.9 %all-gather.4.cloned.1.call-done = bf16[768,1280]{1,0:T(8,128)(2,1)} async-done(((bf16[192,1280]{1,0:T(8,128)(2,1)}), bf16[768,1280]{1,0:T(8,128)(2,1)}) %all-gather.4.cloned.1.call-update) | async-done | bytes 1966096 | tf_op jit(solution)/shard_map/all_gather | solution.py:68
  100.3 6.6 %convolution_convert_fusion.1 = bf16[1280,1280]{1,0:T(8,128)(2,1)} fusion(bf16[768,1280]{1,0:T(8,128)(2,1)} %all-gather.4.cloned.1.call-done, bf16[768,1280]{1,0:T(8,128)(2,1)} %get-tuple-element.30), kind=kOutput, calls=%fused_computation.1 | convolution fusion | flops 2518220800 | bytes 7208960 | tf_op jit(solution)/shard_map/dot_general | solution.py:67
  106.9 0.0 all-reduce.3.cloned.1.call-update
  106.9 0.2 reduce-scatter.2.cloned.1.call-start
  107.2 6.6 %convolution_convert_fusion.2 = bf16[768,1280]{1,0:T(8,128)(2,1)} fusion(bf16[768,1280]{1,0:T(8,128)(2,1)} %get-tuple-element.30, bf16[1280,1280]{1,0:T(8,128)(2,1)} %param.9), kind=kOutput, calls=%fused_computation.44 | convolution fusion | flops 2517565440 | bytes 7208960 | tf_op jit(solution)/shard_map/dot_general | solution.py:56
  113.8 0.0 reduce-scatter.2.cloned.1.call-update
  113.8 14.3 %psum.30 = bf16[1280]{0:T(1024)(128)(2,1)S(1)} all-reduce(bf16[1280]{0:T(1024)(128)(2,1)S(1)} %get-tuple-element.29), channel_id=1, replica_groups=mesh['dp'=8,'tp'=4] {'dp'}, use_global_device_ids=true, to_apply=%region_4.0 | all-reduce | flops 1280 | bytes 5120 | tf_op jit(solution)/shard_map/psum | solution.py:87
  128.1 0.6 convert_element_type.123
  128.7 84.3 %all-reduce.3.cloned.1.call-done = (bf16[1280,1280]{1,0:T(8,128)(2,1)}, bf16[1280,1280]{1,0:T(8,128)(2,1)}) async-done(((bf16[1280,1280]{1,0:T(8,128)(2,1)}, bf16[1280,1280]{1,0:T(8,128)(2,1)}), (bf16[1280,1280]{1,0:T(8,128)(2,1)}, bf16[1280,1280]{1,0:T(8,128)(2,1)})) %all-reduce.3.cloned.1.call-update) | async-done | bytes 6553616 | tf_op jit(solution)/shard_map/psum | solution.py:85
  213.1 0.0 copy-start.2
  213.1 5.4 %convert_element_type.119 = f32[1280,1280]{1,0:T(8,128)} convert(bf16[1280,1280]{1,0:T(8,128)(2,1)} %get-tuple-element.22) | non-fusion elementwise | flops 1638400 | bytes 9830400 | tf_op jit(solution)/shard_map/convert_element_type | solution.py:85
  218.4 0.0 copy-done.2
  218.4 3.3 %convert_element_type.122 = f32[1280,1280]{1,0:T(8,128)} convert(bf16[1280,1280]{1,0:T(8,128)(2,1)S(1)} %copy-done.2) | non-fusion elementwise | flops 1638400 | bytes 9830400 | tf_op jit(solution)/shard_map/convert_element_type | solution.py:86
  221.7 35.3 %reduce-scatter.2.cloned.1.call-done = bf16[192,1280]{1,0:T(8,128)(2,1)} async-done(((bf16[768,1280]{1,0:T(8,128)(2,1)}), bf16[192,1280]{1,0:T(8,128)(2,1)}) %reduce-scatter.2.cloned.1.call-update) | async-done | bytes 491536 | tf_op jit(solution)/shard_map/reduce_scatter | solution.py:55
  257.0 3.8 %fusion.66 = (f32[1280]{0:T(1024)S(1)}, f32[1280]{0:T(1024)S(1)}, f32[1280]{0:T(1024)S(1)}, f32[1280]{0:T(1024)S(1)}, f32[1280]{0:T(1024)S(1)}, /*index=5*/f32[1...) fusion(bf16[3,1280]{1,0:T(4,128)(2,1)S(1)} %collective-permute-done.3, bf16[192,1280]{1,0:T(8,128)(2,1)} %bitcast.132, ...), kind=kLoop, calls=%fused_computation.86 | loop fusion | flops 10804480 | bytes 2508800 | tf_op jit(solution)/shard_map/reduce_sum | solution.py:81
  260.8 0.0 copy-start.3
  260.9 0.7 copy-done.3
  261.6 1.3 collective-permute-start
  262.9 4.5 %collective-permute-start.1 = (bf16[3,1280]{1,0:T(4,128)(2,1)S(1)}, bf16[3,1280]{1,0:T(4,128)(2,1)S(1)}, u32[]{:S(2)}, u32[]{:S(2)}) collective-permute-start(bf16[3,1280]{1,0:T(4,128)(2,1)S(1)} %get-tuple-element.26), channel_id=1, source_target_pairs={{0,1},{1,2},{2,3},{4,5},{5,6},{6,7},{8,9},{9,10},{10,11},{12,13},{... | collective-permute-start | bytes 23048 | tf_op jit(solution)/shard_map/ppermute | solution.py:17
  267.4 0.1 stack.31
  267.5 40.2 %psum.31 = f32[7,1280]{1,0:T(8,128)} all-reduce(f32[7,1280]{1,0:T(8,128)S(1)} %stack.31), channel_id=1, replica_groups=mesh['dp'=8,'tp'=4] {'dp','tp'}, use_global_device_ids=true, to_apply=%region_12.0 | all-reduce | flops 8960 | bytes 71680 | tf_op jit(solution)/shard_map/psum | solution.py:83
  307.6 0.0 collective-permute-done
  307.6 0.0 collective-permute-done.1
  307.6 4.3 %fusion.76 = bf16[1,192,1280]{2,1,0:T(8,128)(2,1)} fusion(bf16[192,1280]{1,0:T(8,128)(2,1)} %copy-done.3, bf16[3,1280]{1,0:T(4,128)(2,1)S(1)} %collective-permute-done.1, f32[1280]{0:T(1024)S(1)} %get-tuple-element.20, f32[1280]{0:T(1024)S(1)} %get-tuple-element.21, f32[1280]{0:T(1024)S(1)} %get-tuple-element.16, f32[1280]{0:T(1024)S(1)} %get-tuple-element.17, ...), kind=kLoop, calls=%fused_computation.109 | loop fusion | flops 9830400 | bytes 1034240 | tf_op jit(solution)/shard_map/broadcast_in_dim | solution.py:89
  (8 shorter events, 0.0 us)
Async XLA Ops:
  7.2 56.6 %copy-start = (bf16[1280,1280]{1,0:T(8,128)(2,1)S(1)}, bf16[1280,1280]{1,0:T(8,128)(2,1)}, u32[]{:S(2)}) copy-start(bf16[1280,1280]{1,0:T(8,128)(2,1)} %param.10) | copy-start | bytes 9830404
  7.2 48.6 %all-gather.6.cloned.1.call-start = ((), (), s32[]{:S(2)}) async-start(), calls=%async_computation.3 | async-start | bytes 2457600 | tf_op jit(solution)/shard_map/all_gather | solution.py:42
  7.9 92.4 %all-gather.4.cloned.1.call-start = ((), (), s32[]{:S(2)}) async-start(), calls=%async_computation.2 | async-start | bytes 2457600 | tf_op jit(solution)/shard_map/all_gather | solution.py:68
  8.9 7.5 %collective-permute-start.2 = (bf16[3,1280]{1,0:T(4,128)(2,1)S(1)}, bf16[3,1280]{1,0:T(4,128)(2,1)S(1)}, u32[]{:S(2)}, u32[]{:S(2)}) collective-permute-start(bf16[3,1280]{1,0:T(4,128)(2,1)S(1)} %get-tuple-element.27), channel_id=1, source_target_pairs={{0,1},{1,2},{2,3},{4,5},{5,6},{6,7},{8,9},{9,10},{10,11},{12,13},{... | collective-permute-start | bytes 23048 | tf_op jit(solution)/shard_map/ppermute | solution.py:17
  13.9 5.6 %collective-permute-start.3 = (bf16[3,1280]{1,0:T(4,128)(2,1)S(1)}, bf16[3,1280]{1,0:T(4,128)(2,1)S(1)}, u32[]{:S(2)}, u32[]{:S(2)}) collective-permute-start(bf16[3,1280]{1,0:T(4,128)(2,1)S(1)} %get-tuple-element.28), channel_id=1, source_target_pairs={{1,0},{2,1},{3,2},{5,4},{6,5},{7,6},{9,8},{10,9},{11,10},{13,12},{... | collective-permute-start | bytes 23048 | tf_op jit(solution)/shard_map/ppermute | solution.py:19
  23.9 189.2 %all-reduce.3.cloned.1.call-start = ((), (), s32[]{:S(2)}) async-start(), calls=%async_computation.4 | async-start | bytes 13107200 | tf_op jit(solution)/shard_map/psum | solution.py:85
  55.8 7.9 %copy-start.1 = (f32[768,1280]{1,0:T(8,128)S(1)}, f32[768,1280]{1,0:T(8,128)}, u32[]{:S(2)}) copy-start(f32[768,1280]{1,0:T(8,128)} %fusion.38) | copy-start | bytes 11796484
  55.8 7.9 %copy-start.4 = (bf16[1,768,1280]{2,1,0:T(8,128)(2,1)S(1)}, bf16[1,768,1280]{2,1,0:T(8,128)(2,1)}, u32[]{:S(2)}) copy-start(bf16[1,768,1280]{2,1,0:T(8,128)(2,1)} %param.7) | copy-start | bytes 5898244
  55.8 7.9 %copy-start.5 = (bf16[1,768,1280]{2,1,0:T(8,128)(2,1)S(1)}, bf16[1,768,1280]{2,1,0:T(8,128)(2,1)}, u32[]{:S(2)}) copy-start(bf16[1,768,1280]{2,1,0:T(8,128)(2,1)} %all-gather.6.cloned.1.call-done) | copy-start | bytes 5898244
  106.9 150.0 %reduce-scatter.2.cloned.1.call-start = ((), (), s32[]{:S(2)}) async-start(), calls=%async_computation.1 | async-start | bytes 2457600 | tf_op jit(solution)/shard_map/reduce_scatter | solution.py:55
  213.1 5.4 %copy-start.2 = (bf16[1280,1280]{1,0:T(8,128)(2,1)S(1)}, bf16[1280,1280]{1,0:T(8,128)(2,1)}, u32[]{:S(2)}) copy-start(bf16[1280,1280]{1,0:T(8,128)(2,1)} %get-tuple-element.23) | copy-start | bytes 9830404
  260.8 0.8 copy-start.3
  261.6 46.1 %collective-permute-start = (bf16[3,1280]{1,0:T(4,128)(2,1)S(1)}, bf16[3,1280]{1,0:T(4,128)(2,1)S(1)}, u32[]{:S(2)}, u32[]{:S(2)}) collective-permute-start(bf16[3,1280]{1,0:T(4,128)(2,1)S(1)} %get-tuple-element.25), channel_id=1, source_target_pairs={{1,0},{2,1},{3,2},{5,4},{6,5},{7,6},{9,8},{10,9},{11,10},{13,12},{... | collective-permute-start | bytes 23048 | tf_op jit(solution)/shard_map/ppermute | solution.py:19
  262.9 44.8 %collective-permute-start.1 = (bf16[3,1280]{1,0:T(4,128)(2,1)S(1)}, bf16[3,1280]{1,0:T(4,128)(2,1)S(1)}, u32[]{:S(2)}, u32[]{:S(2)}) collective-permute-start(bf16[3,1280]{1,0:T(4,128)(2,1)S(1)} %get-tuple-element.26), channel_id=1, source_target_pairs={{0,1},{1,2},{2,3},{4,5},{5,6},{6,7},{8,9},{9,10},{10,11},{12,13},{... | collective-permute-start | bytes 23048 | tf_op jit(solution)/shard_map/ppermute | solution.py:17
Sparse Core Ops, SparseCore 0:
  9.6 46.2 all-gather.5
  58.0 42.3 all-gather.3
  107.1 105.9 all-reduce.2
  215.2 41.6 reduce-scatter.1
where the time goes:
time: 319 us; the launch traced here: 318 us
  waiting for transfers between devices  177 us (55%)
  blocking collectives  54.5 us (17%)
  other arithmetic  31.8 us (10%)
  matrix products  25.8 us (8%)
  between operations  13.9 us (4%)
  starting transfers between devices  12.4 us (4%)
    psum x1, waiting for transfers between devices, shards(): lax.psum(grad_w_in.astype(jnp.bfloat16), 'dp').astype(jnp.float32)  84.3 us
    psum x1, blocking collectives, shards(): grad_kernel = lax.psum(grad_kernel, ('dp', 'tp'))  40.2 us
    reduce_scatter x1, waiting for transfers between devices, shards(): lax.psum_scatter(lax.dot_general(buffer, w_in, (((1,), (1,)), ((), ())),...  35.3 us
    all_gather x1, waiting for transfers between devices, shards(): lax.all_gather(mixed, 'tp', axis=0, tiled=True)  31.9 us
    all_gather x1, waiting for transfers between devices, shards(): piece = lax.all_gather(grad_out, 'tp', axis=0, tiled=True)  21.8 us
    psum x1, blocking collectives, shards(): lax.psum(grad_bias.astype(jnp.bfloat16), 'dp').astype(jnp.float32)  14.3 us
    another operation x1, other arithmetic, gelu_exact(): return jax.nn.gelu(value, approximate=False)  10.1 us
    ppermute x2, starting transfers between devices, with_halo(): lax.ppermute(tail, axis, [(i, (i + 1) % count) for i in range(ends)])  9.5 us
  transfers between devices with their start and end apart: 8, of which 5 were waited for; matrix products, arithmetic and copies ran while one was open for 14% of the time, Pallas kernels for 0%

commit v1 on v0

--- a/solution.py
+++ b/solution.py
@@ -4,6 +4,12 @@
 from jax.sharding import PartitionSpec as P
 
 KW = 7
+
+
+def track_steps_all_for(field_in, a_name, net_axis):
+    for t in (a_name, net_axis):
+        field_in = lax.psum(field_in, t)
+    return field_in
 
 
 def with_halo(cells, sides, width):
@@ -80,7 +86,7 @@
         )
         taps.append(jnp.sum(grad_f * padded[tap : tap + length].astype(jnp.float32), axis=0))
     grad_kernel = jnp.stack(taps)
-    grad_kernel = lax.psum(grad_kernel, ("dp", "tp"))
+    grad_kernel = track_steps_all_for(grad_kernel, "tp", "dp")
     grad_w_in, grad_w_out, grad_bias = (
         lax.psum(grad_w_in.astype(jnp.bfloat16), "dp").astype(jnp.float32),
         lax.psum(grad_w_out.astype(jnp.bfloat16), "dp").astype(jnp.float32),

time: 319 us -> 321 us (level)
    psum x1 -> x2, blocking collectives: 40.2 us -> 41 us  [track_steps_all_for(): field_in = lax.psum(field_in, t)]
where the time goes in v1:
time: 321 us; the launch traced here: 320 us
  waiting for transfers between devices  177 us (55%)
  blocking collectives  55.3 us (17%)
  other arithmetic  32.5 us (10%)
  matrix products  25.8 us (8%)
  between operations  13.9 us (4%)
  starting transfers between devices  12.4 us (4%)
    psum x1, waiting for transfers between devices, shards(): lax.psum(grad_w_in.astype(jnp.bfloat16), 'dp').astype(jnp.float32)  84.3 us
    psum x2, blocking collectives, track_steps_all_for(): field_in = lax.psum(field_in, t)  41 us
    reduce_scatter x1, waiting for transfers between devices, shards(): lax.psum_scatter(lax.dot_general(buffer, w_in, (((1,), (1,)), ((), ())),...  35.3 us
    all_gather x1, waiting for transfers between devices, shards(): lax.all_gather(mixed, 'tp', axis=0, tiled=True)  31.9 us
    all_gather x1, waiting for transfers between devices, shards(): piece = lax.all_gather(grad_out, 'tp', axis=0, tiled=True)  21.8 us
    psum x1, blocking collectives, shards(): lax.psum(grad_bias.astype(jnp.bfloat16), 'dp').astype(jnp.float32)  14.3 us
    another operation x1, other arithmetic, gelu_exact(): return jax.nn.gelu(value, approximate=False)  10.1 us
    ppermute x2, starting transfers between devices, with_halo(): lax.ppermute(tail, axis, [(i, (i + 1) % count) for i in range(ends)])  9.5 us
  transfers between devices with their start and end apart: 8, of which 5 were waited for; matrix products, arithmetic and copies ran while one was open for 14% of the time, Pallas kernels for 0%

profile of v1, /device:TPU:0, one launch (start us, length us, event | category | flops | bytes accessed | tf_op | source)
XLA Modules:
  0.0 320.1 jit_solution(2717562579214316680)
XLA Ops:
  7.2 0.0 copy-start
  7.2 0.0 all-gather.6.cloned.1.call-start
  7.2 0.7 all-gather.6.cloned.1.call-update
  7.9 0.0 all-gather.4.cloned.1.call-start
  8.0 1.0 slice_bitcast_fusion.1
  8.9 5.0 %collective-permute-start.2 = (bf16[3,1280]{1,0:T(4,128)(2,1)S(1)}, bf16[3,1280]{1,0:T(4,128)(2,1)S(1)}, u32[]{:S(2)}, u32[]{:S(2)}) collective-permute-start(bf16[3,1280]{1,0:T(4,128)(2,1)S(1)} %get-tuple-element.27), channel_id=1, source_target_pairs={{0,1},{1,2},{2,3},{4,5},{5,6},{6,7},{8,9},{9,10},{10,11},{12,13},{... | collective-permute-start | bytes 23048 | tf_op jit(solution)/shard_map/ppermute | solution.py:23
  13.9 1.3 collective-permute-start.3
  15.2 1.3 slice_reduce_fusion.6
  16.4 0.0 collective-permute-done.2
  16.5 3.0 collective-permute-done.3
  19.4 4.4 %fusion.52 = bf16[192,1280]{1,0:T(8,128)(2,1)} fusion(bf16[192,1280]{1,0:T(8,128)(2,1)} %bitcast.131, bf16[3,1280]{1,0:T(4,128)(2,1)S(1)} %collective-permute-done.3, bf16[3,1280]{1,0:T(4,128)(2,1)S(1)} %collective-permute-done.2, f32[1280]{0:T(1024)S(1)} %get-tuple-element.20, f32[1280]{0:T(1024)S(1)} %get-tuple-element.21, f32[1280]{0:T(1024)S(1)} %get-tuple-element.16, ...), kind=kLoop, calls=%fused_computation.72 | loop fusion | flops 9830400 | bytes 1034240 | tf_op jit(solution)/shard_map/convert_element_type | solution.py:40
  23.8 0.0 all-gather.4.cloned.1.call-update
  23.9 0.0 all-reduce.3.cloned.1.call-start
  23.9 10.1 %fusion.38 = f32[768,1280]{1,0:T(8,128)} fusion(bf16[1,768,1280]{2,1,0:T(8,128)(2,1)} %param.7), kind=kLoop, calls=%fused_computation.43 | loop fusion | flops 61931520 | bytes 5898240 | tf_op jit(solution)/shard_map/jvp()/erfc | solution.py:33
  34.0 21.8 %all-gather.6.cloned.1.call-done = bf16[1,768,1280]{2,1,0:T(8,128)(2,1)} async-done(((bf16[1,192,1280]{2,1,0:T(8,128)(2,1)}), bf16[1,768,1280]{2,1,0:T(8,128)(2,1)}) %all-gather.6.cloned.1.call-update) | async-done | bytes 1966096 | tf_op jit(solution)/shard_map/all_gather | solution.py:48
  55.8 0.0 copy-start.1
  55.8 0.0 copy-start.3
  55.8 0.0 copy-start.4
  55.8 7.9 %convolution_convert_fusion = bf16[1280,1280]{1,0:T(8,128)(2,1)} fusion(f32[768,1280]{1,0:T(8,128)} %fusion.38, bf16[1,768,1280]{2,1,0:T(8,128)(2,1)} %param.7, bf16[1,768,1280]{2,1,0:T(8,128)(2,1)} %all-gather.6.cloned.1.call-done), kind=kOutput, calls=%fused_computation | convolution fusion | flops 2522152960 | bytes 11141120 | tf_op jit(solution)/shard_map/dot_general | solution.py:56
  63.7 0.0 copy-done
  63.7 0.0 copy-done.1
  63.7 0.0 copy-done.3
  63.7 0.0 copy-done.4
  63.8 4.7 %fusion.80 = (bf16[1280]{0:T(1024)(128)(2,1)S(1)}, bf16[768,1280]{1,0:T(8,128)(2,1)}) fusion(f32[768,1280]{1,0:T(8,128)S(1)} %copy-done.1, bf16[1280,1280]{1,0:T(8,128)(2,1)S(1)} %copy-done, bf16[1,768,1280]{2,1,0:T(8,128)(2,1)S(1)} %copy-done.4, bf16[1,768,1280]{2,1,0:T(8,128)(2,1)S(1)} %copy-done.3), kind=kOutput, calls=%fused_computation.121 | convolution fusion | flops 2532309760 | bytes 13109760 | tf_op jit(solution)/shard_map/dot_general | solution.py:50
  68.5 31.9 %all-gather.4.cloned.1.call-done = bf16[768,1280]{1,0:T(8,128)(2,1)} async-done(((bf16[192,1280]{1,0:T(8,128)(2,1)}), bf16[768,1280]{1,0:T(8,128)(2,1)}) %all-gather.4.cloned.1.call-update) | async-done | bytes 1966096 | tf_op jit(solution)/shard_map/all_gather | solution.py:74
  100.3 6.6 %convolution_convert_fusion.1 = bf16[1280,1280]{1,0:T(8,128)(2,1)} fusion(bf16[768,1280]{1,0:T(8,128)(2,1)} %all-gather.4.cloned.1.call-done, bf16[768,1280]{1,0:T(8,128)(2,1)} %get-tuple-element.30), kind=kOutput, calls=%fused_computation.1 | convolution fusion | flops 2518220800 | bytes 7208960 | tf_op jit(solution)/shard_map/dot_general | solution.py:73
  106.9 0.0 all-reduce.3.cloned.1.call-update
  106.9 0.2 reduce-scatter.2.cloned.1.call-start
  107.2 6.6 %convolution_convert_fusion.2 = bf16[768,1280]{1,0:T(8,128)(2,1)} fusion(bf16[768,1280]{1,0:T(8,128)(2,1)} %get-tuple-element.30, bf16[1280,1280]{1,0:T(8,128)(2,1)} %param.9), kind=kOutput, calls=%fused_computation.44 | convolution fusion | flops 2517565440 | bytes 7208960 | tf_op jit(solution)/shard_map/dot_general | solution.py:62
  113.8 0.0 reduce-scatter.2.cloned.1.call-update
  113.8 14.3 %psum.37 = bf16[1280]{0:T(1024)(128)(2,1)S(1)} all-reduce(bf16[1280]{0:T(1024)(128)(2,1)S(1)} %get-tuple-element.29), channel_id=1, replica_groups=mesh['dp'=8,'tp'=4] {'dp'}, use_global_device_ids=true, to_apply=%region_4.0 | all-reduce | flops 1280 | bytes 5120 | tf_op jit(solution)/shard_map/psum | solution.py:93
  128.1 0.6 convert_element_type.123
  128.7 84.3 %all-reduce.3.cloned.1.call-done = (bf16[1280,1280]{1,0:T(8,128)(2,1)}, bf16[1280,1280]{1,0:T(8,128)(2,1)}) async-done(((bf16[1280,1280]{1,0:T(8,128)(2,1)}, bf16[1280,1280]{1,0:T(8,128)(2,1)}), (bf16[1280,1280]{1,0:T(8,128)(2,1)}, bf16[1280,1280]{1,0:T(8,128)(2,1)})) %all-reduce.3.cloned.1.call-update) | async-done | bytes 6553616 | tf_op jit(solution)/shard_map/psum | solution.py:91
  213.1 0.0 copy-start.2
  213.1 5.4 %convert_element_type.119 = f32[1280,1280]{1,0:T(8,128)} convert(bf16[1280,1280]{1,0:T(8,128)(2,1)} %get-tuple-element.22) | non-fusion elementwise | flops 1638400 | bytes 9830400 | tf_op jit(solution)/shard_map/convert_element_type | solution.py:91
  218.4 0.0 copy-done.2
  218.4 3.3 %convert_element_type.122 = f32[1280,1280]{1,0:T(8,128)} convert(bf16[1280,1280]{1,0:T(8,128)(2,1)S(1)} %copy-done.2) | non-fusion elementwise | flops 1638400 | bytes 9830400 | tf_op jit(solution)/shard_map/convert_element_type | solution.py:92
  221.7 35.3 %reduce-scatter.2.cloned.1.call-done = bf16[192,1280]{1,0:T(8,128)(2,1)} async-done(((bf16[768,1280]{1,0:T(8,128)(2,1)}), bf16[192,1280]{1,0:T(8,128)(2,1)}) %reduce-scatter.2.cloned.1.call-update) | async-done | bytes 491536 | tf_op jit(solution)/shard_map/reduce_scatter | solution.py:61
  257.0 4.4 %fusion.66 = (f32[1280]{0:T(1024)S(1)}, f32[1280]{0:T(1024)S(1)}, f32[1280]{0:T(1024)S(1)}, f32[1280]{0:T(1024)S(1)}, f32[1280]{0:T(1024)S(1)}, /*index=5*/f32[1...) fusion(bf16[3,1280]{1,0:T(4,128)(2,1)S(1)} %collective-permute-done.3, bf16[192,1280]{1,0:T(8,128)(2,1)} %bitcast.132, ...), kind=kLoop, calls=%fused_computation.86 | loop fusion | flops 10804480 | bytes 2508800 | tf_op jit(solution)/shard_map/reduce_sum | solution.py:87
  261.5 0.1 stack.31
  261.6 17.7 %psum.38 = f32[7,1280]{1,0:T(8,128)S(1)} all-reduce(f32[7,1280]{1,0:T(8,128)S(1)} %stack.31), channel_id=1, replica_groups=mesh['dp'=8,'tp'=4] {'tp'}, use_global_device_ids=true, to_apply=%region_12.0 | all-reduce | flops 8960 | bytes 71680 | tf_op jit(solution)/shard_map/psum | solution.py:11
  279.3 0.8 fusion.79
  280.1 1.3 collective-permute-start
  281.4 4.5 %collective-permute-start.1 = (bf16[3,1280]{1,0:T(4,128)(2,1)S(1)}, bf16[3,1280]{1,0:T(4,128)(2,1)S(1)}, u32[]{:S(2)}, u32[]{:S(2)}) collective-permute-start(bf16[3,1280]{1,0:T(4,128)(2,1)S(1)} %get-tuple-element.26), channel_id=1, source_target_pairs={{0,1},{1,2},{2,3},{4,5},{5,6},{6,7},{8,9},{9,10},{10,11},{12,13},{... | collective-permute-start | bytes 23048 | tf_op jit(solution)/shard_map/ppermute | solution.py:23
  285.9 23.3 %psum.39 = f32[7,1280]{1,0:T(8,128)} all-reduce(f32[7,1280]{1,0:T(8,128)S(1)} %psum.38), channel_id=1, replica_groups=mesh['dp'=8,'tp'=4] {'dp'}, use_global_device_ids=true, to_apply=%region_13.0 | all-reduce | flops 8960 | bytes 71680 | tf_op jit(solution)/shard_map/psum | solution.py:11
  309.2 0.0 collective-permute-done
  309.2 0.0 collective-permute-done.1
  309.2 4.3 %fusion.76 = bf16[1,192,1280]{2,1,0:T(8,128)(2,1)} fusion(bf16[192,1280]{1,0:T(8,128)(2,1)} %get-tuple-element.24, bf16[3,1280]{1,0:T(4,128)(2,1)S(1)} %collective-permute-done.1, f32[1280]{0:T(1024)S(1)} %get-tuple-element.20, f32[1280]{0:T(1024)S(1)} %get-tuple-element.21, f32[1280]{0:T(1024)S(1)} %get-tuple-element.16, f32[1280]{0:T(1024)S(1)} %get-tuple-element.17, ...), kind=kLoop, calls=%fused_computation.109 | loop fusion | flops 9830400 | bytes 1034240 | tf_op jit(solution)/shard_map/broadcast_in_dim | solution.py:95
  (7 shorter events, 0.0 us)
Async XLA Ops:
  7.2 56.6 %copy-start = (bf16[1280,1280]{1,0:T(8,128)(2,1)S(1)}, bf16[1280,1280]{1,0:T(8,128)(2,1)}, u32[]{:S(2)}) copy-start(bf16[1280,1280]{1,0:T(8,128)(2,1)} %param.10) | copy-start | bytes 9830404
  7.2 48.6 %all-gather.6.cloned.1.call-start = ((), (), s32[]{:S(2)}) async-start(), calls=%async_computation.3 | async-start | bytes 2457600 | tf_op jit(solution)/shard_map/all_gather | solution.py:48
  7.9 92.4 %all-gather.4.cloned.1.call-start = ((), (), s32[]{:S(2)}) async-start(), calls=%async_computation.2 | async-start | bytes 2457600 | tf_op jit(solution)/shard_map/all_gather | solution.py:74
  8.9 7.5 %collective-permute-start.2 = (bf16[3,1280]{1,0:T(4,128)(2,1)S(1)}, bf16[3,1280]{1,0:T(4,128)(2,1)S(1)}, u32[]{:S(2)}, u32[]{:S(2)}) collective-permute-start(bf16[3,1280]{1,0:T(4,128)(2,1)S(1)} %get-tuple-element.27), channel_id=1, source_target_pairs={{0,1},{1,2},{2,3},{4,5},{5,6},{6,7},{8,9},{9,10},{10,11},{12,13},{... | collective-permute-start | bytes 23048 | tf_op jit(solution)/shard_map/ppermute | solution.py:23
  13.9 5.6 %collective-permute-start.3 = (bf16[3,1280]{1,0:T(4,128)(2,1)S(1)}, bf16[3,1280]{1,0:T(4,128)(2,1)S(1)}, u32[]{:S(2)}, u32[]{:S(2)}) collective-permute-start(bf16[3,1280]{1,0:T(4,128)(2,1)S(1)} %get-tuple-element.28), channel_id=1, source_target_pairs={{1,0},{2,1},{3,2},{5,4},{6,5},{7,6},{9,8},{10,9},{11,10},{13,12},{... | collective-permute-start | bytes 23048 | tf_op jit(solution)/shard_map/ppermute | solution.py:25
  23.9 189.2 %all-reduce.3.cloned.1.call-start = ((), (), s32[]{:S(2)}) async-start(), calls=%async_computation.4 | async-start | bytes 13107200 | tf_op jit(solution)/shard_map/psum | solution.py:91
  55.8 7.9 %copy-start.1 = (f32[768,1280]{1,0:T(8,128)S(1)}, f32[768,1280]{1,0:T(8,128)}, u32[]{:S(2)}) copy-start(f32[768,1280]{1,0:T(8,128)} %fusion.38) | copy-start | bytes 11796484
  55.8 7.9 %copy-start.3 = (bf16[1,768,1280]{2,1,0:T(8,128)(2,1)S(1)}, bf16[1,768,1280]{2,1,0:T(8,128)(2,1)}, u32[]{:S(2)}) copy-start(bf16[1,768,1280]{2,1,0:T(8,128)(2,1)} %param.7) | copy-start | bytes 5898244
  55.8 7.9 %copy-start.4 = (bf16[1,768,1280]{2,1,0:T(8,128)(2,1)S(1)}, bf16[1,768,1280]{2,1,0:T(8,128)(2,1)}, u32[]{:S(2)}) copy-start(bf16[1,768,1280]{2,1,0:T(8,128)(2,1)} %all-gather.6.cloned.1.call-done) | copy-start | bytes 5898244
  106.9 150.0 %reduce-scatter.2.cloned.1.call-start = ((), (), s32[]{:S(2)}) async-start(), calls=%async_computation.1 | async-start | bytes 2457600 | tf_op jit(solution)/shard_map/reduce_scatter | solution.py:61
  213.1 5.4 %copy-start.2 = (bf16[1280,1280]{1,0:T(8,128)(2,1)S(1)}, bf16[1280,1280]{1,0:T(8,128)(2,1)}, u32[]{:S(2)}) copy-start(bf16[1280,1280]{1,0:T(8,128)(2,1)} %get-tuple-element.23) | copy-start | bytes 9830404
  280.1 29.2 %collective-permute-start = (bf16[3,1280]{1,0:T(4,128)(2,1)S(1)}, bf16[3,1280]{1,0:T(4,128)(2,1)S(1)}, u32[]{:S(2)}, u32[]{:S(2)}) collective-permute-start(bf16[3,1280]{1,0:T(4,128)(2,1)S(1)} %get-tuple-element.25), channel_id=1, source_target_pairs={{1,0},{2,1},{3,2},{5,4},{6,5},{7,6},{9,8},{10,9},{11,10},{13,12},{... | collective-permute-start | bytes 23048 | tf_op jit(solution)/shard_map/ppermute | solution.py:25
  281.4 27.9 %collective-permute-start.1 = (bf16[3,1280]{1,0:T(4,128)(2,1)S(1)}, bf16[3,1280]{1,0:T(4,128)(2,1)S(1)}, u32[]{:S(2)}, u32[]{:S(2)}) collective-permute-start(bf16[3,1280]{1,0:T(4,128)(2,1)S(1)} %get-tuple-element.26), channel_id=1, source_target_pairs={{0,1},{1,2},{2,3},{4,5},{5,6},{6,7},{8,9},{9,10},{10,11},{12,13},{... | collective-permute-start | bytes 23048 | tf_op jit(solution)/shard_map/ppermute | solution.py:23
Sparse Core Ops, SparseCore 0:
  9.6 46.2 all-gather.5
  58.0 42.3 all-gather.3
  107.1 105.9 all-reduce.2
  215.2 41.6 reduce-scatter.1
